TPU v7x, 32 devices: a whole 2x2x4 slice. The times are simulated.
32 devices in a mesh: pipe: 4 (over y, x), dp: 8 (over z, core).
Axes of the slice: x: 2, y: 2, z: 4, core: 2. Of those that a mesh axis runs over, the one named last changes fastest.
Arguments:
- acts: bfloat16 [4, 2048, 3072], P('pipe', 'dp'), may hold values from -24 to 24, as said below
- grad: float32 [12288, 4096], P('pipe', 'dp'), may hold values from -6 to 6
- owner_of: int32 [4, 12], replicated, may hold values from 0 to 3, as said below
Outputs:
- precond: float32 [12288, 4096], P('pipe', 'dp')
- held_inverse: float32 [4, 24, 256, 256], P('pipe', None, 'dp')
Inputs may be any that keep to these rules, and one draw needn't show every extreme that they name: `acts`: column and token scales of the activations vary; entries lie within the range. `owner_of`: no section index owns more than 24 blocks in all, and some section index owns exactly 24.
All inputs are finite; a program needn't handle non-finite values.
Results may differ from a plain program's by a relative error of at most 0.0003.
Values sent between devices are 32-bit elements; how exact they have to be, the bound alone decides.
A program may use at most 128 MiB of HBM per device.

v0:
```python
import jax
import jax.numpy as jnp
from jax import lax
from jax.sharding import PartitionSpec as P

BLK = 256
HOST = 24


damping_ratio = 0.1


def invert_blocks(factor, vacant):
    order_size = factor.shape[-1]
    diagonal_sum = jnp.sum(jnp.diagonal(factor, axis1=1, axis2=2), axis=1)
    damping = damping_ratio * diagonal_sum / order_size
    identity = jnp.eye(order_size, dtype=factor.dtype)
    shifted = factor + (damping + vacant)[:, None, None] * identity
    cholesky_lower = jnp.linalg.cholesky(shifted)
    identity_stack = jnp.broadcast_to(identity, factor.shape)
    inv_lower = lax.linalg.triangular_solve(
        cholesky_lower, identity_stack, left_side=True, lower=True
    )
    return jnp.einsum("mkr,mkc->mrc", inv_lower, inv_lower, precision=lax.Precision.HIGHEST)


def slot_tables(owner_of):
    owners_flat = owner_of.reshape(-1)
    positions = jnp.arange(owners_flat.shape[0], dtype=jnp.int32)
    matches = owners_flat[:, None] == owners_flat[None, :]
    before = positions[None, :] < positions[:, None]
    slot_rank = jnp.sum((matches & before).astype(jnp.int32), axis=1)
    return (owners_flat, slot_rank)


def shards(acts, grad, owner_of):
    tokens = acts.shape[1]
    feature_count = acts.shape[2]
    nblocks = feature_count // BLK
    data_count = lax.axis_size("dp")
    section_count = lax.axis_size("pipe")
    row_share = BLK // data_count
    all_tokens = tokens * data_count
    section_index = lax.axis_index("pipe")
    member = lax.axis_index("dp")
    features = acts[0].reshape(tokens, nblocks, BLK)
    owners_flat, slot_rank = slot_tables(owner_of)
    slot_ids = jnp.arange(HOST, dtype=jnp.int32)
    pick_mine = (
        (owners_flat[None, :] == section_index) & (slot_rank[None, :] == slot_ids[:, None])
    ).astype(jnp.float32)
    own_owners = lax.dynamic_index_in_dim(owner_of, section_index, 0, keepdims=False)
    own_ranks = lax.dynamic_index_in_dim(
        slot_rank.reshape(section_count, nblocks), section_index, 0, keepdims=False
    )
    target = own_owners * HOST + own_ranks
    pick_back = (
        jnp.arange(section_count * HOST, dtype=jnp.int32)[None, :] == target[:, None]
    ).astype(jnp.float32)
    block_terms = jnp.einsum("tbr,tbc->rbc", features, features, preferred_element_type=jnp.float32)
    my_rows = lax.psum_scatter(
        block_terms.reshape(row_share * lax.axis_size("dp"), nblocks * BLK),
        "dp",
        scatter_dimension=0,
        tiled=True,
    )
    pieces = lax.all_gather(my_rows, "pipe", axis=0, tiled=True).reshape(
        section_count, row_share, nblocks, BLK
    )
    hosted = jnp.einsum(
        "jsb,srbc->jrc",
        pick_mine.reshape(HOST, section_count, nblocks),
        pieces,
        precision=lax.Precision.HIGHEST,
    )
    occupied = jnp.sum(pick_mine, axis=1)
    per_member = (HOST + data_count - 1) // data_count
    padded_count = per_member * data_count
    padded = jnp.pad(hosted, ((0, padded_count - HOST), (0, 0), (0, 0)))
    mine_blocks = lax.all_to_all(padded, "dp", split_axis=0, concat_axis=1, tiled=True) / all_tokens
    padded_flags = jnp.pad(occupied, (0, padded_count - HOST))
    held_flags = lax.dynamic_slice_in_dim(padded_flags, member * per_member, per_member, 0)
    inverted = invert_blocks(mine_blocks, 1.0 - held_flags) * held_flags[:, None, None]
    spread_rows = lax.all_to_all(inverted, "dp", split_axis=1, concat_axis=0, tiled=True)
    held_rows = spread_rows[:HOST]
    returned = lax.all_gather(held_rows, "pipe", axis=0, tiled=True)
    own_rows = jnp.einsum("bm,mrc->brc", pick_back, returned, precision=lax.Precision.HIGHEST)
    inverse = lax.all_gather(own_rows, "dp", axis=1, tiled=True)
    grad_blocks = grad.reshape(nblocks, BLK, grad.shape[1])
    precond = jnp.einsum("brk,bkc->brc", inverse, grad_blocks, precision=lax.Precision.HIGHEST)
    return (precond.reshape(feature_count, grad.shape[1]), held_rows[None])


def solution(mesh):
    placed = (P("pipe", "dp", None), P("pipe", "dp"), P())
    return jax.shard_map(
        shards,
        mesh=mesh,
        in_specs=placed,
        out_specs=(P("pipe", "dp"), P("pipe", None, "dp", None)),
        check_vma=False,
    )
```

profile of v0, /device:TPU:25, one launch (start us, length us, event | category | flops | bytes accessed | tf_op | source)
XLA Modules:
  0.0 444.1 jit_solution(14781126711529102693)
XLA Ops:
  7.2 0.0 reduce-scatter.2.cloned.1.call-start
  7.2 1.7 copy.123
  8.9 2.3 fusion.30
  11.2 3.5 copy.125
  14.7 0.0 reduce-scatter.2.cloned.1.call-update
  14.7 0.0 all-gather.4.cloned.1.call-start
  14.8 40.4 %reduce-scatter.2.cloned.1.call-done = f32[32,3072]{1,0:T(8,128)} async-done(((f32[256,3072]{1,0:T(8,128)}), f32[32,3072]{1,0:T(8,128)}) %reduce-scatter.2.cloned.1.call-update) | async-done | bytes 393232 | tf_op jit(solution)/shard_map/reduce_scatter | solution.py:61
  55.2 0.1 eq.76
  55.3 0.2 convert_reduce_fusion
  55.5 0.1 reshape.93
  55.6 32.5 %all-gather.4.cloned.1.call-done = f32[128,3072]{1,0:T(8,128)} async-done(((f32[32,3072]{1,0:T(8,128)}), f32[128,3072]{1,0:T(8,128)}) %all-gather.4.cloned.1.call-update) | async-done | bytes 1572880 | tf_op jit(solution)/shard_map/all_gather | solution.py:67
  88.0 1.7 reshape.95
  89.8 0.9 convolution_bitcast_fusion
  90.7 1.1 copy.127
  91.8 5.5 %all-to-all-start = ((f32[24,32,256]{2,1,0:T(8,128)}), f32[24,32,256]{2,1,0:T(8,128)S(1)}, u32[]{:S(2)}, u32[]{:S(2)}) async-start(f32[24,32,256]{2,1,0:T(8,128)} %copy.127), calls=%async_computation.1 | async-start | bytes 1572864 | tf_op jit(solution)/shard_map/all_to_all | solution.py:80
  97.4 0.7 copy.135
  98.1 0.1 copy.137
  98.2 0.5 iota_multiply_fusion
  98.8 0.1 convert_reduce_fusion.1
  98.9 0.6 iota_compare_fusion.2
  99.6 0.6 iota_compare_fusion.1
  100.2 15.5 %all-to-all-done = f32[24,32,256]{2,1,0:T(8,128)S(1)} async-done(((f32[24,32,256]{2,1,0:T(8,128)}), f32[24,32,256]{2,1,0:T(8,128)S(1)}, u32[]{:S(2)}, u32[]{:S(2)}) %all-to-all-start) | async-done | bytes 786464 | tf_op jit(solution)/shard_map/all_to_all | solution.py:80
  115.7 0.1 broadcast_multiply_fusion
  115.8 0.1 copy.128
  115.8 16.8 %copy.129 = f32[3,256,256]{0,2,1:T(8,128)} copy(f32[3,256,256]{2,1,0:T(8,128)S(1)} %bitcast.75) | data formatting | bytes 1572864 | tf_op jit(solution)/shard_map/div | solution.py:80
  132.6 0.3 copy.130
  132.9 2.3 gather_fusion
  135.2 0.1 reduce_sum.28
  135.3 0.6 subtract_add_fusion
  135.9 0.5 copy-done.4
  136.4 0.1 multiply_add_fusion
  136.5 0.3 copy.131
  136.8 0.8 fusion.5
  137.7 35.2 %custom-call.16 = f32[3,128,128]{2,1,0:T(8,128)S(1)} custom-call(f32[3,128,128]{2,1,0:T(8,128)S(1)} %cholesky.122), custom_call_target="Cholesky" | custom-call | tf_op jit(solution)/shard_map/jit(cholesky)/cholesky | solution.py:19
  172.9 0.1 cholesky.117
  173.0 0.8 select_bitcast_fusion
  173.7 29.5 %custom-call.17 = f32[3,1,128,128]{2,3,1,0:T(8,128)S(1)} custom-call(f32[3,1,128,128]{3,2,1,0:T(8,128)S(1)} %select_bitcast_fusion), custom_call_target="InvertDiagBlocksLowerTriangular" | custom-call | tf_op jit(solution)/shard_map/jit(cholesky)/cholesky | solution.py:19
  203.2 0.3 constant_dynamic-update-slice_fusion.1
  203.6 0.5 convolution_subtract_fusion.1
  204.1 35.4 %custom-call.18 = f32[3,128,128]{2,1,0:T(8,128)S(1)} custom-call(f32[3,128,128]{2,1,0:T(8,128)S(1)} %convolution_subtract_fusion.1), custom_call_target="Cholesky" | custom-call | tf_op jit(solution)/shard_map/jit(cholesky)/cholesky | solution.py:19
  239.6 0.1 compare_reduce_fusion
  239.7 0.2 select_select_fusion
  239.9 0.1 triangular_solve.69
  240.0 5.4 %while.1 = (s32[]{:T(128)}, f32[3,256,256]{2,1,0:T(8,128)S(1)}, s32[2,2]{1,0:T(2,128)S(1)}, f32[2,3,128,128]{3,2,0,1:T(8,128)}, s32[]{:T(128)}) while((s32[]{:T(128)}, f32[3,256,256]{2,1,0:T(8,128)S(1)}, s32[2,2]{1,0:T(2,128)S(1)}, f32[2,3,128,128]{3,2,0,1:T(8,128)}, s32[]{:T(128)}) %tuple.29), condition=%wide.while_cond, body=%wide.while_body.sunk | while | flops 2 | bytes 394849 | solution.py:21
  240.0 0.6 fusion.42
  240.6 2.1 bitcast_dynamic-update-slice_fusion.2
  242.7 0.6 fusion.42
  243.3 2.1 bitcast_dynamic-update-slice_fusion.2
  245.4 59.8 %custom-call.19 = f32[3,2,128,128]{2,3,1,0:T(8,128)S(1)} custom-call(f32[3,2,128,128]{3,2,1,0:T(8,128)} %bitcast.83), custom_call_target="InvertDiagBlocksLowerTriangular" | custom-call | tf_op jit(solution)/shard_map/triangular_solve | solution.py:21
  305.2 0.5 fusion.9
  305.7 0.5 convolution_subtract_fusion
  306.2 0.5 fusion.8
  306.7 1.4 convolution_multiply_fusion
  308.2 0.5 copy.140
  308.7 29.0 %all_to_all.27 = f32[3,256,256]{2,0,1:T(4,128)S(1)} all-to-all(f32[3,256,256]{2,0,1:T(4,128)S(1)} %copy.140), channel_id=1, replica_groups=mesh['pipe'=4,'dp'=8] {'dp'}, dimensions={1} | all-to-all | bytes 1572864 | tf_op jit(solution)/shard_map/all_to_all | solution.py:84
  337.7 0.2 copy.141
  337.8 1.0 copy.142
  338.8 0.3 all-gather.8.cloned.1.call-start
  339.1 0.7 fusion.26
  339.8 42.6 %all-gather.6.cloned.1.call-done = f32[96,32,256]{2,1,0:T(8,128)} async-done(((f32[24,32,256]{2,1,0:T(8,128)}), f32[96,32,256]{2,1,0:T(8,128)}) %all-gather.6.cloned.1.call-update) | async-done | bytes 3145744 | tf_op jit(solution)/shard_map/all_gather | solution.py:86
  382.4 4.7 %fusion = f32[12,32,256]{2,0,1:T(8,128)S(1)} fusion(f32[96,32,256]{2,1,0:T(8,128)} %all-gather.6.cloned.1.call-done, s32[12]{0:T(128)S(1)} %fusion.26), kind=kOutput, calls=%fused_computation.3 | convolution fusion | flops 113247360 | bytes 3538992 | tf_op jit(solution)/shard_map/bm,mrc->brc/dot_general | solution.py:87
  387.1 1.0 copy.144
  388.1 36.9 %all-gather.8.cloned.1.call-done = f32[12,256,256]{2,1,0:T(8,128)} async-done(((f32[12,32,256]{2,1,0:T(8,128)}), f32[12,256,256]{2,1,0:T(8,128)}) %all-gather.8.cloned.1.call-update) | async-done | bytes 3145744 | tf_op jit(solution)/shard_map/all_gather | solution.py:88
  425.0 12.5 %fusion.31 = f32[12,256,512]{2,1,0:T(8,128)} fusion(f32[12,256,256]{2,1,0:T(8,128)} %all-gather.8.cloned.1.call-done, f32[12,256,512]{2,1,0:T(8,128)} %bitcast.77), kind=kOutput, calls=%fused_computation.66 | convolution fusion | flops 4831838208 | bytes 15728640 | tf_op jit(solution)/shard_map/brk,bkc->brc/dot_general | solution.py:90
  (29 shorter events, 0.2 us)
Async XLA Ops:
  7.2 48.0 %reduce-scatter.2.cloned.1.call-start = ((), (), s32[]{:S(2)}) async-start(), calls=%async_computation.3 | async-start | bytes 3538944 | tf_op jit(solution)/shard_map/reduce_scatter | solution.py:61
  14.7 40.5 %copy-start.2 = (s32[4,12]{1,0:T(4,128)S(1)}, s32[4,12]{1,0:T(4,128)}, u32[]{:S(2)}) copy-start(s32[4,12]{1,0:T(4,128)} %param.5) | copy-start | bytes 580
  14.7 73.3 %all-gather.4.cloned.1.call-start = ((), (), s32[]{:S(2)}) async-start(), calls=%async_computation.4 | async-start | bytes 1966080 | tf_op jit(solution)/shard_map/all_gather | solution.py:67
  55.6 35.1 %copy-start.3 = (s32[4,12]{1,0:T(4,128)}, s32[4,12]{1,0:T(4,128)S(1)}, u32[]{:S(2)}) copy-start(s32[4,12]{1,0:T(4,128)S(1)} %reshape.93) | copy-start | bytes 580
  91.8 23.9 %all-to-all-start = ((f32[24,32,256]{2,1,0:T(8,128)}), f32[24,32,256]{2,1,0:T(8,128)S(1)}, u32[]{:S(2)}, u32[]{:S(2)}) async-start(f32[24,32,256]{2,1,0:T(8,128)} %copy.127), calls=%async_computation.1 | async-start | bytes 1572864 | tf_op jit(solution)/shard_map/all_to_all | solution.py:80
  97.3 285.1 %all-gather.6.cloned.1.call-start = ((), (), s32[]{:S(2)}) async-start(), calls=%async_computation.5 | async-start | bytes 3932160 | tf_op jit(solution)/shard_map/all_gather | solution.py:86
  135.9 0.5 copy-start.4
  136.8 102.9 %copy-start.1 = (pred[256,256]{1,0:T(8,128)(4,1)S(1)}, pred[256,256]{1,0:T(8,128)(4,1)}, u32[]{:S(2)}) copy-start(pred[256,256]{1,0:T(8,128)(4,1)} %iota_compare_fusion.1) | copy-start | bytes 196612
  137.7 102.3 %copy-start.6 = (s32[2]{0:T(128)S(1)}, s32[2]{0:T(128)}, u32[]{:S(2)}) copy-start(s32[2]{0:T(128)} %iota_multiply_fusion) | copy-start | bytes 28
  172.9 132.2 %copy-start = (f32[128,256]{1,0:T(8,128)S(1)}, f32[128,256]{1,0:T(8,128)}, u32[]{:S(2)}) copy-start(f32[128,256]{1,0:T(8,128)} %copy.135) | copy-start | bytes 393220
  239.7 67.0 %copy-start.5 = (f32[3]{0:T(128)S(1)}, f32[3]{0:T(128)}, u32[]{:S(2)}) copy-start(f32[3]{0:T(128)} %get-tuple-element.21) | copy-start | bytes 40
  338.8 86.2 %all-gather.8.cloned.1.call-start = ((), (), s32[]{:S(2)}) async-start(), calls=%async_computation.6 | async-start | bytes 3538944 | tf_op jit(solution)/shard_map/all_gather | solution.py:88
Sparse Core Ops, SparseCore 0:
  14.9 40.2 reduce-scatter.1
  57.0 31.0 all-gather.3
  338.9 43.4 all-gather.5
  388.2 36.7 all-gather.7
where the time goes:
time: 448 us; the launch traced here: 444 us
  waiting for transfers between devices  168 us (38%)
  other arithmetic  165 us (37%)
  local copies, waits for them, and re-layouts  37.5 us (8%)
  blocking collectives  29 us (6%)
  matrix products  24.2 us (5%)
  between operations  14.1 us (3%)
  starting transfers between devices  5.93 us (1%)
    another operation x9, other arithmetic, invert_blocks(): cholesky_lower = jnp.linalg.cholesky(shifted)  102 us
    another operation x4, other arithmetic, invert_blocks(): lax.linalg.triangular_solve(cholesky_lower, identity_stack, left_side=Tru...  61.1 us
    all_gather x1, waiting for transfers between devices, shards(): returned = lax.all_gather(held_rows, 'pipe', axis=0, tiled=True)  42.6 us
    reduce_scatter x1, waiting for transfers between devices, shards(): lax.psum_scatter(block_terms.reshape(row_share * lax.axis_size('dp'), nbl...  40.4 us
    all_gather x1, waiting for transfers between devices, shards(): inverse = lax.all_gather(own_rows, 'dp', axis=1, tiled=True)  36.9 us
    all_gather x1, waiting for transfers between devices, shards(): lax.all_gather(my_rows, 'pipe', axis=0, tiled=True)  32.5 us
    all_to_all x1, blocking collectives, shards(): lax.all_to_all(inverted, 'dp', split_axis=1, concat_axis=0, tiled=True)  29 us
    div x3, local copies, waits for them, and re-layouts, shards(): lax.all_to_all(padded, 'dp', split_axis=0, concat_axis=1, tiled=True)  17.1 us
  transfers between devices with their start and end apart: 5, of which 5 were waited for; matrix products, arithmetic and copies ran while one was open for 1% of the time, Pallas kernels for 0%

commit v1 on v0

v1 whole, which is shorter than its diff:
```python
import functools

import jax
import jax.numpy as jnp
from jax import lax
from jax.experimental import pallas as pl
from jax.experimental.pallas import tpu as pltpu
from jax.sharding import PartitionSpec as P

BLK = 256
HALF = BLK // 2
PACK = HALF + 8
HOST = 24
MESH = pl.DeviceIdType.MESH

damping_ratio = 0.1
F32 = jnp.float32
BF16 = jnp.bfloat16
HIGHEST = lax.Precision.HIGHEST


def square_iota():
    rows = lax.broadcasted_iota(jnp.int32, (HALF, HALF), 0)
    cols = lax.broadcasted_iota(jnp.int32, (HALF, HALF), 1)
    return rows, cols


def pack_into(ref, m11, m21, m22):
    rows, cols = square_iota()
    diag = jnp.sum(jnp.where(rows == cols, m22, 0.0), axis=0, keepdims=True)
    ref[0:HALF, 0:HALF] = m21
    ref[0:HALF, HALF:BLK] = jnp.where(rows >= cols, m11, m22)
    ref[HALF:PACK, 0:HALF] = jnp.broadcast_to(diag, (PACK - HALF, HALF))
    ref[HALF:PACK, HALF:BLK] = jnp.zeros((PACK - HALF, HALF), F32)


def unpack(value):
    rows, cols = square_iota()
    m21 = value[0:HALF, 0:HALF]
    mixed = value[0:HALF, HALF:BLK]
    diag = value[HALF : HALF + 1, 0:HALF]
    turned = mixed.T
    m11 = jnp.where(rows >= cols, mixed, turned)
    m22 = jnp.where(rows < cols, mixed, jnp.where(rows == cols, diag, turned))
    return m11, m21, m22


def reduce_kernel(n, nhalf, nown, acts, out, theirs, mine, from_pair, from_chip, pair_s, pair_r, chip_s, chip_r):
    chips = n // 2
    me = lax.axis_index("dp")
    core = lax.rem(me, 2)
    chip = me // 2
    pair = me + 1 - 2 * core

    barrier = pltpu.get_barrier_semaphore()
    pl.semaphore_signal(barrier, inc=1, device_id={"dp": pair}, device_id_type=MESH)
    for step in range(1, chips):
        other = lax.rem(chip + step, chips) * 2 + core
        pl.semaphore_signal(barrier, inc=1, device_id={"dp": other}, device_id_type=MESH)
    pl.semaphore_wait(barrier, chips)

    def partial(block, ref):
        start = pl.multiple_of(block * BLK, BLK)
        x = acts[:, pl.ds(start, BLK)]
        full = lax.dot_general(x, x, (((0,), (0,)), ((), ())), preferred_element_type=F32)
        pack_into(ref, full[0:HALF, 0:HALF], full[HALF:BLK, 0:HALF], full[HALF:BLK, HALF:BLK])

    def pair_copy(t):
        return pltpu.make_async_remote_copy(
            src_ref=theirs.at[t], dst_ref=from_pair.at[t], send_sem=pair_s.at[t], recv_sem=pair_r.at[t],
            device_id={"dp": pair}, device_id_type=MESH,
        )

    @pl.loop(0, nhalf)
    def _(t):
        partial(2 * t + 1 - core, theirs.at[t])
        pair_copy(t).start()

    @pl.loop(0, nhalf)
    def _(t):
        partial(2 * t + core, mine.at[t])

    def chip_copy(t, slot, owner):
        return pltpu.make_async_remote_copy(
            src_ref=mine.at[t], dst_ref=from_chip.at[slot, chip], send_sem=chip_s.at[t],
            recv_sem=chip_r.at[slot, chip], device_id={"dp": owner * 2 + core}, device_id_type=MESH,
        )

    for t in range(nhalf):
        owner = t % chips
        pair_copy(t).wait()
        mine[t] = mine[t] + from_pair[t]

        @pl.when(chip != owner)
        def _():
            chip_copy(t, t // chips, owner).start()

    for slot in range(nown):
        t = slot * chips + chip

        @pl.when(t < nhalf)
        def _():
            total = mine[t]
            for step in range(1, chips):
                source = lax.rem(chip + step, chips)
                pltpu.make_async_remote_copy(
                    src_ref=from_chip.at[slot, source], dst_ref=from_chip.at[slot, source],
                    send_sem=chip_s.at[0], recv_sem=chip_r.at[slot, source],
                    device_id={"dp": source * 2 + core}, device_id_type=MESH,
                ).wait_recv()
                total = total + from_chip[slot, source]
            out[slot] = total

        @pl.when(t >= nhalf)
        def _():
            rows, cols = square_iota()
            eye = jnp.where(rows == cols, 1.0, 0.0)
            pack_into(out.at[slot], eye, jnp.zeros((HALF, HALF), F32), eye)

    for t in range(nhalf):
        owner = t % chips

        @pl.when(chip != owner)
        def _():
            chip_copy(t, t // chips, owner).wait_send()


def dot3(a, b, contract):
    return jnp.stack([
        lax.dot_general(a[i], b[i], (contract, ((), ())), precision=HIGHEST, preferred_element_type=F32)
        for i in range(a.shape[0])
    ])


def sweep_inverse(a):
    count = a.shape[0]
    panel_shape = (count, 8, HALF)
    sub = lax.broadcasted_iota(jnp.int32, panel_shape, 1)
    lane = lax.broadcasted_iota(jnp.int32, panel_shape, 2)
    all_lanes = lax.broadcasted_iota(jnp.int32, (count, HALF, HALF), 2)

    def panel(_, a):
        top = a[:, 0:8, :]
        cols = [jnp.broadcast_to(top[:, :, k : k + 1], panel_shape) for k in range(8)]
        lead = [jnp.broadcast_to(a[:, :, k : k + 1], a.shape) for k in range(8)]
        for k in range(8):
            here = cols[k]
            inv = jnp.broadcast_to(1.0 / here[:, k : k + 1, :], panel_shape)
            row = jnp.broadcast_to(top[:, k : k + 1, :], panel_shape) * inv
            at_row = sub == k
            new = jnp.where(at_row, row, top - here * row)
            edge = jnp.where(at_row, inv, -here * inv)
            top = jnp.where(lane == k, edge, new)
            for j in range(k + 1, 8):
                across = jnp.broadcast_to(cols[j][:, k : k + 1, :], panel_shape) * inv
                cols[j] = jnp.where(at_row, across, cols[j] - here * across)
        top = jnp.where(lane < 8, -top, top)
        rest = a
        for k in range(8):
            rest = rest - lead[k] * top[:, k : k + 1, :]
        tall = jnp.concatenate([top, jnp.zeros((count, HALF - 8, HALF), F32)], axis=1)
        turned = jnp.stack([tall[i].T for i in range(count)])
        rest = jnp.where(all_lanes < 8, turned, rest)
        a = jnp.concatenate([rest[:, 8:, :], top], axis=1)
        return pltpu.roll(a, HALF - 8, 2)

    return -lax.fori_loop(0, HALF // 8, panel, a)


def invert_kernel(tokens, packed, out):
    count = packed.shape[0]
    rows, cols = square_iota()
    parts = [unpack(packed[i] / tokens) for i in range(count)]
    m11 = jnp.stack([p[0] for p in parts])
    m21 = jnp.stack([p[1] for p in parts])
    m22 = jnp.stack([p[2] for p in parts])
    eye = rows == cols
    trace = jnp.sum(jnp.where(eye, m11 + m22, 0.0), axis=(1, 2), keepdims=True)
    damping = jnp.where(eye, damping_ratio * trace / BLK, 0.0)
    x11 = sweep_inverse(m11 + damping)
    g = dot3(m21, x11, ((1,), (0,)))
    schur = m22 + damping - dot3(g, m21, ((1,), (1,)))
    y = sweep_inverse(schur)
    b21 = -dot3(y, g, ((1,), (0,)))
    b11 = x11 - dot3(g, b21, ((0,), (0,)))
    for i in range(count):
        pack_into(out.at[i], b11[i], b21[i], y[i])


def spread_kernel(n, sections, nhalf, nown, packed, full, rows_out, landed, near_s, near_r, pair_s, side_s, side_r):
    chips = n // 2
    share = BLK // n
    me = lax.axis_index("dp")
    section = lax.axis_index("pipe")
    core = lax.rem(me, 2)
    chip = me // 2
    pair = me + 1 - 2 * core

    barrier = pltpu.get_barrier_semaphore()
    pl.semaphore_signal(barrier, inc=1, device_id={"dp": pair}, device_id_type=MESH)
    for step in range(1, chips):
        other = lax.rem(chip + step, chips) * 2 + core
        pl.semaphore_signal(barrier, inc=1, device_id={"dp": other}, device_id_type=MESH)
    for step in range(1, sections):
        pl.semaphore_signal(
            barrier, inc=1, device_id={"pipe": lax.rem(section + step, sections)}, device_id_type=MESH
        )
    pl.semaphore_wait(barrier, chips + sections - 1)

    def send(source, block, target, sem):
        return pltpu.make_async_remote_copy(
            src_ref=source, dst_ref=landed.at[block], send_sem=sem, recv_sem=near_r.at[block],
            device_id={"dp": target}, device_id_type=MESH,
        )

    def side(block, step):
        mine = full.at[block, pl.ds(pl.multiple_of(me * share, share), share), :]
        return pltpu.make_async_remote_copy(
            src_ref=mine, dst_ref=rows_out.at[section, block], send_sem=side_s.at[block, step - 1],
            recv_sem=side_r.at[section, block],
            device_id={"pipe": lax.rem(section + step, sections)}, device_id_type=MESH,
        )

    def open_block(value, block):
        m11, m21, m22 = unpack(value)
        full[block, 0:HALF, 0:HALF] = m11
        full[block, HALF:BLK, 0:HALF] = m21
        full[block, 0:HALF, HALF:BLK] = m21.T
        full[block, HALF:BLK, HALF:BLK] = m22
        for step in range(1, sections):
            side(block, step).start()
        rows_out[section, block] = full[block, pl.ds(pl.multiple_of(me * share, share), share), :]

    for slot in range(nown):
        t = slot * chips + chip

        @pl.when(t < nhalf)
        def _():
            for step in range(1, chips):
                send(packed.at[slot], 2 * t + core, lax.rem(chip + step, chips) * 2 + core, near_s.at[slot, step - 1]).start()
            send(packed.at[slot], 2 * t + core, pair, pair_s.at[t]).start()

    for slot in range(nown):
        t = slot * chips + chip

        @pl.when(t < nhalf)
        def _():
            open_block(packed[slot], 2 * t + core)

    def arrived(block):
        send(landed.at[block], block, pair, pair_s.at[0]).wait_recv()

    for t in range(nhalf):
        @pl.when(chip != t % chips)
        def _():
            block = 2 * t + core
            arrived(block)
            send(landed.at[block], block, pair, pair_s.at[t]).start()
            open_block(landed[block], block)

        block = 2 * t + 1 - core
        arrived(block)
        open_block(landed[block], block)

    for slot in range(nown):
        t = slot * chips + chip

        @pl.when(t < nhalf)
        def _():
            for step in range(1, chips):
                send(packed.at[slot], 2 * t + core, lax.rem(chip + step, chips) * 2 + core, near_s.at[slot, step - 1]).wait_send()

    for t in range(nhalf):
        send(landed.at[2 * t + core], 2 * t + core, pair, pair_s.at[t]).wait_send()

    @pl.loop(0, 2 * nhalf)
    def _(block):
        for step in range(1, sections):
            side(block, step).wait_send()
            source = lax.rem(section + step, sections)
            pltpu.make_async_remote_copy(
                src_ref=rows_out.at[source, block], dst_ref=rows_out.at[source, block],
                send_sem=side_s.at[block, step - 1], recv_sem=side_r.at[source, block],
                device_id={"pipe": source}, device_id_type=MESH,
            ).wait_recv()


def apply_kernel(per_step, owners, inverse, grad, rows, precond, held, slots):
    step = pl.program_id(0)
    section = lax.axis_index("pipe")
    sections, nblocks = owners.shape
    total = sections * nblocks

    @pl.when(step == 0)
    def _():
        for j in range(HOST):
            slots[j] = -1

        def place(k, used):
            hit = owners[k // nblocks, lax.rem(k, nblocks)] == section

            @pl.when(hit)
            def _():
                slots[used] = k

            return used + hit.astype(jnp.int32)

        lax.fori_loop(0, total, place, jnp.int32(0))

    for j in range(per_step):
        k = slots[step * per_step + j]
        at = jnp.maximum(k, 0)
        value = rows[at // nblocks, lax.rem(at, nblocks)]
        held[j] = jnp.where(k >= 0, value, 0.0)

    a = inverse[0]
    b = grad[...]
    a_high = a.astype(BF16)
    a_low = (a - a_high.astype(F32)).astype(BF16)
    b_high = b.astype(BF16)
    b_low = (b - b_high.astype(F32)).astype(BF16)
    small = jnp.dot(a_high, b_low, preferred_element_type=F32) + jnp.dot(a_low, b_high, preferred_element_type=F32)
    precond[...] = jnp.dot(a_high, b_high, preferred_element_type=F32) + small


def shards(acts, grad, owner_of):
    tokens, feature_count = acts.shape[1:]
    columns = grad.shape[1]
    nblocks = feature_count // BLK
    n = lax.axis_size("dp")
    sections = lax.axis_size("pipe")
    chips = n // 2
    nhalf = nblocks // 2
    nown = -(-nhalf // chips)
    share = BLK // n
    vmem = pl.BlockSpec(memory_space=pltpu.VMEM)
    dma = pltpu.SemaphoreType.DMA
    limit = 56 * 1024 * 1024

    summed = pl.pallas_call(
        functools.partial(reduce_kernel, n, nhalf, nown),
        out_shape=jax.ShapeDtypeStruct((nown, PACK, BLK), F32),
        in_specs=[vmem],
        out_specs=vmem,
        scratch_shapes=[
            pltpu.VMEM((nhalf, PACK, BLK), F32),
            pltpu.VMEM((nhalf, PACK, BLK), F32),
            pltpu.VMEM((nhalf, PACK, BLK), F32),
            pltpu.VMEM((nown, chips, PACK, BLK), F32),
            dma((nhalf,)), dma((nhalf,)), dma((nhalf,)), dma((nown, chips)),
        ],
        compiler_params=pltpu.CompilerParams(collective_id=0, has_side_effects=True),
        name="reduce_factors",
    )(acts[0])

    packed = pl.pallas_call(
        functools.partial(invert_kernel, float(tokens * n)),
        out_shape=jax.ShapeDtypeStruct((nown, PACK, BLK), F32),
        in_specs=[vmem],
        out_specs=vmem,
        name="invert_blocks",
    )(summed)

    inverse, rows = pl.pallas_call(
        functools.partial(spread_kernel, n, sections, nhalf, nown),
        out_shape=(
            jax.ShapeDtypeStruct((nblocks, BLK, BLK), F32),
            jax.ShapeDtypeStruct((sections, nblocks, share, BLK), F32),
        ),
        in_specs=[vmem],
        out_specs=(vmem, vmem),
        scratch_shapes=[
            pltpu.VMEM((nblocks, PACK, BLK), F32),
            dma((nown, chips - 1)), dma((nblocks,)), dma((nhalf,)),
            dma((nblocks, sections - 1)), dma((sections, nblocks)),
        ],
        compiler_params=pltpu.CompilerParams(collective_id=1, has_side_effects=True),
        name="spread_inverses",
    )(packed)

    per_step = HOST // nblocks
    precond, held = pl.pallas_call(
        functools.partial(apply_kernel, per_step),
        grid_spec=pltpu.PrefetchScalarGridSpec(
            num_scalar_prefetch=1,
            grid=(nblocks,),
            in_specs=[
                pl.BlockSpec((1, BLK, BLK), lambda i, o: (i, 0, 0)),
                pl.BlockSpec((BLK, columns), lambda i, o: (i, 0)),
                pl.BlockSpec((sections, nblocks, share, BLK), lambda i, o: (0, 0, 0, 0), pipeline_mode=pl.Buffered(1)),
            ],
            out_specs=[
                pl.BlockSpec((BLK, columns), lambda i, o: (i, 0)),
                pl.BlockSpec((per_step, share, BLK), lambda i, o: (i, 0, 0)),
            ],
            scratch_shapes=[pltpu.SMEM((HOST,), jnp.int32)],
        ),
        out_shape=(
            jax.ShapeDtypeStruct((feature_count, columns), F32),
            jax.ShapeDtypeStruct((HOST, share, BLK), F32),
        ),
        compiler_params=pltpu.CompilerParams(dimension_semantics=("arbitrary",)),
        name="apply_inverses",
    )(owner_of, inverse, grad, rows)
    return precond, held[None]


def solution(mesh):
    placed = (P("pipe", "dp", None), P("pipe", "dp"), P())
    return jax.shard_map(
        shards,
        mesh=mesh,
        in_specs=placed,
        out_specs=(P("pipe", "dp"), P("pipe", None, "dp", None)),
        check_vma=False,
    )
```

time: 448 us -> 110 us (0.25)
  waiting for transfers between devices: 168 us -> 0 us
  other arithmetic: 165 us -> 0 us
  Pallas kernels: 0 us -> 109 us
  local copies, waits for them, and re-layouts: 37.5 us -> 0 us
  blocking collectives: 29 us -> 0 us
  matrix products: 24.2 us -> 0 us
  between operations: 14.1 us -> 0.65 us
  starting transfers between devices: 5.93 us -> 0 us
    another operation x13 -> x0, other arithmetic: 163 us -> none  [the longest x9 102 us: invert_blocks(): cholesky_lower = jnp.linalg.cholesky(shifted)]
    all_gather x3 -> x0, waiting for transfers between devices: 112 us -> none  [the longest x1 42.6 us: shards(): returned = lax.all_gather(held_rows, 'pipe', axis=0, tiled=True)]
    pallas_call x0 -> x4, Pallas kernels: none -> 109 us  [the longest x1 52.6 us: shards(): pl.pallas_call(functools.partial(spread_kernel, n, sections, nhalf, nown)...]
    reduce_scatter x1 -> x0, waiting for transfers between devices: 40.4 us -> none  [shards(): lax.psum_scatter(block_terms.reshape(row_share * lax.axis_size('dp'), nbl...]
    all_to_all x1 -> x0, blocking collectives: 29 us -> none  [shards(): lax.all_to_all(inverted, 'dp', split_axis=1, concat_axis=0, tiled=True)]
    dot_general x5 -> x0, matrix products: 21.8 us -> none  [the longest x1 12.5 us: shards(): jnp.einsum('brk,bkc->brc', inverse, grad_blocks, precision=lax.Precision....]
    div x3 -> x0, local copies, waits for them, and re-layouts: 17.1 us -> none  [shards(): lax.all_to_all(padded, 'dp', split_axis=0, concat_axis=1, tiled=True)]
    all_to_all x1 -> x0, waiting for transfers between devices: 15.5 us -> none  [shards(): lax.all_to_all(padded, 'dp', split_axis=0, concat_axis=1, tiled=True)]
  transfers between devices with their start and end apart: 5 -> 0, of which waited for: 5 -> 0; matrix products, arithmetic and copies ran while one was open for 1% -> 0% of each run, Pallas kernels for 0% -> 0%
where the time goes in v1:
time: 110 us; the launch traced here: 109 us
  Pallas kernels  109 us (99%)
    pallas_call x1, Pallas kernels, shards(): pl.pallas_call(functools.partial(spread_kernel, n, sections, nhalf, nown)...  52.6 us
    pallas_call x1, Pallas kernels, shards(): pl.pallas_call(functools.partial(invert_kernel, float(tokens * n)), out_s...  22.2 us
    pallas_call x1, Pallas kernels, shards(): pl.pallas_call(functools.partial(reduce_kernel, n, nhalf, nown), out_shap...  20.7 us
    pallas_call x1, Pallas kernels, shards(): pl.pallas_call(functools.partial(apply_kernel, per_step), grid_spec=pltpu...  13.1 us

profile of v1, /device:TPU:25, one launch (start us, length us, event | category | flops | bytes accessed | tf_op | source)
XLA Modules:
  0.0 109.2 jit_solution(15539764378073125413)
XLA Ops:
  0.6 20.7 %reduce_factors.1.packed = f32[2,136,256]{2,1,0:T(8,128)} custom-call(bf16[256,3072]{1,0:T(8,128)(2,1)} %bitcast.2), custom_call_target="tpu_custom_call" | custom-call | tf_op jit(solution)/shard_map/reduce_factors/pallas_call | solution.py:340
  21.3 22.2 %invert_blocks.1.packed = f32[2,136,256]{2,1,0:T(8,128)} custom-call(f32[2,136,256]{2,1,0:T(8,128)} %reduce_factors.1.packed), custom_call_target="tpu_custom_call" | custom-call | tf_op jit(solution)/shard_map/invert_blocks/pallas_call | solution.py:356
  43.5 52.6 %spread_inverses.1 = (f32[12,256,256]{2,1,0:T(8,128)}, f32[4,12,32,256]{3,2,1,0:T(8,128)}) custom-call(f32[2,136,256]{2,1,0:T(8,128)} %invert_blocks.1.packed), custom_call_target="tpu_custom_call" | custom-call | tf_op jit(solution)/shard_map/spread_inverses/pallas_call | solution.py:364
  96.1 13.1 %apply_inverses.1 = (f32[3072,512]{1,0:T(8,128)}, f32[24,32,256]{2,1,0:T(8,128)}) custom-call(s32[4,12]{1,0:T(4,128)} %owners.1, f32[12,256,256]{2,1,0:T(8,128)} %get-tuple-element.6.inverse, f32[3072,512]{1,0:T(8,128)} %grad.1, f32[4,12,32,256]{3,2,1,0:T(8,128)} %get-tuple-element.7.rows), custom_call_target="tpu_custom_call" | custom-call | tf_op jit(solution)/shard_map/apply_inverses/pallas_call | solution.py:382

commit v2 on v1

--- a/solution.py
+++ b/solution.py
@@ -45,19 +45,42 @@
     return m11, m21, m22
 
 
-def reduce_kernel(n, nhalf, nown, acts, out, theirs, mine, from_pair, from_chip, pair_s, pair_r, chip_s, chip_r):
+def owner_plan(chips, nhalf):
+    order = []
+    for i in range((chips + 1) // 2):
+        order.extend([i] if i == chips - 1 - i else [i, chips - 1 - i])
+    return [order[t % chips] for t in range(nhalf)], [order.index(i) for i in range(chips)]
+
+
+def look_up(table, index):
+    return sum((index == i).astype(jnp.int32) * value for i, value in enumerate(table))
+
+
+def greet(signals):
+    barrier = pltpu.get_barrier_semaphore()
+    for condition, device in signals:
+        if condition is None:
+            pl.semaphore_signal(barrier, inc=1, device_id=device, device_id_type=MESH)
+        else:
+            @pl.when(condition)
+            def _():
+                pl.semaphore_signal(barrier, inc=1, device_id=device, device_id_type=MESH)
+    peers = sum(1 if condition is None else condition.astype(jnp.int32) for condition, _ in signals)
+    pl.semaphore_wait(barrier, peers)
+
+
+def reduce_kernel(n, nhalf, nown, acts, out, theirs, mine, from_pair, from_low, from_high,
+                  pair_s, pair_r, line_s, low_r, high_r):
     chips = n // 2
     me = lax.axis_index("dp")
     core = lax.rem(me, 2)
     chip = me // 2
     pair = me + 1 - 2 * core
-
-    barrier = pltpu.get_barrier_semaphore()
-    pl.semaphore_signal(barrier, inc=1, device_id={"dp": pair}, device_id_type=MESH)
-    for step in range(1, chips):
-        other = lax.rem(chip + step, chips) * 2 + core
-        pl.semaphore_signal(barrier, inc=1, device_id={"dp": other}, device_id_type=MESH)
-    pl.semaphore_wait(barrier, chips)
+    low = (jnp.maximum(chip - 1, 0)) * 2 + core
+    high = (jnp.minimum(chip + 1, chips - 1)) * 2 + core
+    owners, places = owner_plan(chips, nhalf)
+
+    greet([(None, {"dp": pair}), (chip > 0, {"dp": low}), (chip < chips - 1, {"dp": high})])
 
     def partial(block, ref):
         start = pl.multiple_of(block * BLK, BLK)
@@ -80,36 +103,69 @@
     def _(t):
         partial(2 * t + core, mine.at[t])
 
-    def chip_copy(t, slot, owner):
-        return pltpu.make_async_remote_copy(
-            src_ref=mine.at[t], dst_ref=from_chip.at[slot, chip], send_sem=chip_s.at[t],
-            recv_sem=chip_r.at[slot, chip], device_id={"dp": owner * 2 + core}, device_id_type=MESH,
-        )
-
-    for t in range(nhalf):
-        owner = t % chips
+    @pl.loop(0, nhalf)
+    def _(t):
         pair_copy(t).wait()
         mine[t] = mine[t] + from_pair[t]
 
-        @pl.when(chip != owner)
-        def _():
-            chip_copy(t, t // chips, owner).start()
-
+    def upward(t):
+        return pltpu.make_async_remote_copy(
+            src_ref=mine.at[t], dst_ref=from_low.at[t], send_sem=line_s.at[t], recv_sem=low_r.at[t],
+            device_id={"dp": high}, device_id_type=MESH,
+        )
+
+    def downward(t):
+        return pltpu.make_async_remote_copy(
+            src_ref=mine.at[t], dst_ref=from_high.at[t], send_sem=line_s.at[t], recv_sem=high_r.at[t],
+            device_id={"dp": low}, device_id_type=MESH,
+        )
+
+    up = sorted((t for t in range(nhalf) if owners[t] > 0), key=lambda t: -owners[t])
+    down = sorted((t for t in range(nhalf) if owners[t] < chips - 1), key=lambda t: owners[t])
+
+    @pl.loop(0, nhalf + chips - 1)
+    def _(tick):
+        i = tick - chip
+        t = look_up(up, i)
+
+        @pl.when((i >= 0) & (i < len(up)) & (look_up(owners, t) > chip))
+        def _():
+            @pl.when(chip > 0)
+            def _():
+                upward(t).wait_recv()
+                mine[t] = mine[t] + from_low[t]
+
+            upward(t).start()
+
+        j = tick - (chips - 1 - chip)
+        u = look_up(down, j)
+
+        @pl.when((j >= 0) & (j < len(down)) & (look_up(owners, u) < chip))
+        def _():
+            @pl.when(chip < chips - 1)
+            def _():
+                downward(u).wait_recv()
+                mine[u] = mine[u] + from_high[u]
+
+            downward(u).start()
+
+    place = look_up(places, chip)
     for slot in range(nown):
-        t = slot * chips + chip
+        t = slot * chips + place
 
         @pl.when(t < nhalf)
         def _():
-            total = mine[t]
-            for step in range(1, chips):
-                source = lax.rem(chip + step, chips)
-                pltpu.make_async_remote_copy(
-                    src_ref=from_chip.at[slot, source], dst_ref=from_chip.at[slot, source],
-                    send_sem=chip_s.at[0], recv_sem=chip_r.at[slot, source],
-                    device_id={"dp": source * 2 + core}, device_id_type=MESH,
-                ).wait_recv()
-                total = total + from_chip[slot, source]
-            out[slot] = total
+            out[slot] = mine[t]
+
+            @pl.when(chip > 0)
+            def _():
+                upward(t).wait_recv()
+                out[slot] = out[slot] + from_low[t]
+
+            @pl.when(chip < chips - 1)
+            def _():
+                downward(t).wait_recv()
+                out[slot] = out[slot] + from_high[t]
 
         @pl.when(t >= nhalf)
         def _():
@@ -118,11 +174,9 @@
             pack_into(out.at[slot], eye, jnp.zeros((HALF, HALF), F32), eye)
 
     for t in range(nhalf):
-        owner = t % chips
-
-        @pl.when(chip != owner)
-        def _():
-            chip_copy(t, t // chips, owner).wait_send()
+        @pl.when(chip != owners[t])
+        def _():
+            upward(t).wait_send()
 
 
 def dot3(a, b, contract):
@@ -187,7 +241,7 @@
         pack_into(out.at[i], b11[i], b21[i], y[i])
 
 
-def spread_kernel(n, sections, nhalf, nown, packed, full, rows_out, landed, near_s, near_r, pair_s, side_s, side_r):
+def spread_kernel(n, sections, nhalf, nown, packed, full, rows_out, landed, low_s, high_s, near_r, pair_s, side_s, side_r):
     chips = n // 2
     share = BLK // n
     me = lax.axis_index("dp")
@@ -195,21 +249,19 @@
     core = lax.rem(me, 2)
     chip = me // 2
     pair = me + 1 - 2 * core
-
-    barrier = pltpu.get_barrier_semaphore()
-    pl.semaphore_signal(barrier, inc=1, device_id={"dp": pair}, device_id_type=MESH)
-    for step in range(1, chips):
-        other = lax.rem(chip + step, chips) * 2 + core
-        pl.semaphore_signal(barrier, inc=1, device_id={"dp": other}, device_id_type=MESH)
-    for step in range(1, sections):
-        pl.semaphore_signal(
-            barrier, inc=1, device_id={"pipe": lax.rem(section + step, sections)}, device_id_type=MESH
-        )
-    pl.semaphore_wait(barrier, chips + sections - 1)
-
-    def send(source, block, target, sem):
+    low = (jnp.maximum(chip - 1, 0)) * 2 + core
+    high = (jnp.minimum(chip + 1, chips - 1)) * 2 + core
+    owners, places = owner_plan(chips, nhalf)
+
+    greet(
+        [(None, {"dp": pair}), (chip > 0, {"dp": low}), (chip < chips - 1, {"dp": high})]
+        + [(None, {"pipe": lax.rem(section + step, sections)}) for step in range(1, sections)]
+    )
+
+    def send(source, t, half, target, sem):
+        block = 2 * t + half
         return pltpu.make_async_remote_copy(
-            src_ref=source, dst_ref=landed.at[block], send_sem=sem, recv_sem=near_r.at[block],
+            src_ref=source, dst_ref=landed.at[block], send_sem=sem.at[t], recv_sem=near_r.at[block],
             device_id={"dp": target}, device_id_type=MESH,
         )
 
@@ -231,47 +283,91 @@
             side(block, step).start()
         rows_out[section, block] = full[block, pl.ds(pl.multiple_of(me * share, share), share), :]
 
+    place = look_up(places, chip)
     for slot in range(nown):
-        t = slot * chips + chip
+        t = slot * chips + place
 
         @pl.when(t < nhalf)
         def _():
-            for step in range(1, chips):
-                send(packed.at[slot], 2 * t + core, lax.rem(chip + step, chips) * 2 + core, near_s.at[slot, step - 1]).start()
-            send(packed.at[slot], 2 * t + core, pair, pair_s.at[t]).start()
+            @pl.when(chip > 0)
+            def _():
+                send(packed.at[slot], t, core, low, low_s).start()
+
+            @pl.when(chip < chips - 1)
+            def _():
+                send(packed.at[slot], t, core, high, high_s).start()
+
+            send(packed.at[slot], t, core, pair, pair_s).start()
+
+    def arrived(t, half):
+        send(landed.at[2 * t + half], t, half, pair, pair_s).wait_recv()
+
+    def receive(t):
+        arrived(t, core)
+        source = landed.at[2 * t + core]
+
+        @pl.when((look_up(owners, t) > chip) & (chip > 0))
+        def _():
+            send(source, t, core, low, low_s).start()
+
+        @pl.when((look_up(owners, t) < chip) & (chip < chips - 1))
+        def _():
+            send(source, t, core, high, high_s).start()
+
+        send(source, t, core, pair, pair_s).start()
 
     for slot in range(nown):
-        t = slot * chips + chip
+        t = slot * chips + place
 
         @pl.when(t < nhalf)
         def _():
             open_block(packed[slot], 2 * t + core)
-
-    def arrived(block):
-        send(landed.at[block], block, pair, pair_s.at[0]).wait_recv()
+            other = 2 * t + 1 - core
+            arrived(t, 1 - core)
+            open_block(landed[other], other)
+
+    from_high = sorted(range(nhalf), key=lambda t: owners[t])
+    from_low = sorted(range(nhalf), key=lambda t: -owners[t])
+    below = sum((chip >= owner).astype(jnp.int32) for owner in owners)
+    above = sum((chip <= owner).astype(jnp.int32) for owner in owners)
+
+    @pl.loop(0, nhalf)
+    def _(tick):
+        i = tick + below
+        t = look_up(from_high, i)
+        j = tick + above
+        u = look_up(from_low, j)
+
+        @pl.when(i < nhalf)
+        def _():
+            receive(t)
+
+        @pl.when(j < nhalf)
+        def _():
+            receive(u)
+
+        for half in (core, 1 - core):
+            for use, which in ((i < nhalf, t), (j < nhalf, u)):
+                @pl.when(use)
+                def _():
+                    block = 2 * which + half
+                    if half is not core:
+                        arrived(which, half)
+                    open_block(landed[block], block)
 
     for t in range(nhalf):
-        @pl.when(chip != t % chips)
-        def _():
-            block = 2 * t + core
-            arrived(block)
-            send(landed.at[block], block, pair, pair_s.at[t]).start()
-            open_block(landed[block], block)
-
-        block = 2 * t + 1 - core
-        arrived(block)
-        open_block(landed[block], block)
-
-    for slot in range(nown):
-        t = slot * chips + chip
-
-        @pl.when(t < nhalf)
-        def _():
-            for step in range(1, chips):
-                send(packed.at[slot], 2 * t + core, lax.rem(chip + step, chips) * 2 + core, near_s.at[slot, step - 1]).wait_send()
-
-    for t in range(nhalf):
-        send(landed.at[2 * t + core], 2 * t + core, pair, pair_s.at[t]).wait_send()
+        owner = owners[t]
+        source = landed.at[2 * t + core]
+
+        @pl.when((chip > 0) & (chip <= owner))
+        def _():
+            send(source, t, core, low, low_s).wait_send()
+
+        @pl.when((chip < chips - 1) & (chip >= owner))
+        def _():
+            send(source, t, core, high, high_s).wait_send()
+
+        send(source, t, core, pair, pair_s).wait_send()
 
     @pl.loop(0, 2 * nhalf)
     def _(block):
@@ -313,14 +409,16 @@
         value = rows[at // nblocks, lax.rem(at, nblocks)]
         held[j] = jnp.where(k >= 0, value, 0.0)
 
-    a = inverse[0]
-    b = grad[...]
-    a_high = a.astype(BF16)
-    a_low = (a - a_high.astype(F32)).astype(BF16)
-    b_high = b.astype(BF16)
-    b_low = (b - b_high.astype(F32)).astype(BF16)
-    small = jnp.dot(a_high, b_low, preferred_element_type=F32) + jnp.dot(a_low, b_high, preferred_element_type=F32)
-    precond[...] = jnp.dot(a_high, b_high, preferred_element_type=F32) + small
+    for i in range(inverse.shape[0]):
+        span = slice(i * BLK, (i + 1) * BLK)
+        a = inverse[i]
+        b = grad[span, :]
+        a_high = a.astype(BF16)
+        a_low = (a - a_high.astype(F32)).astype(BF16)
+        b_high = b.astype(BF16)
+        b_low = (b - b_high.astype(F32)).astype(BF16)
+        small = jnp.dot(a_high, b_low, preferred_element_type=F32) + jnp.dot(a_low, b_high, preferred_element_type=F32)
+        precond[span, :] = jnp.dot(a_high, b_high, preferred_element_type=F32) + small
 
 
 def shards(acts, grad, owner_of):
@@ -335,7 +433,6 @@
     share = BLK // n
     vmem = pl.BlockSpec(memory_space=pltpu.VMEM)
     dma = pltpu.SemaphoreType.DMA
-    limit = 56 * 1024 * 1024
 
     summed = pl.pallas_call(
         functools.partial(reduce_kernel, n, nhalf, nown),
@@ -346,8 +443,9 @@
             pltpu.VMEM((nhalf, PACK, BLK), F32),
             pltpu.VMEM((nhalf, PACK, BLK), F32),
             pltpu.VMEM((nhalf, PACK, BLK), F32),
-            pltpu.VMEM((nown, chips, PACK, BLK), F32),
-            dma((nhalf,)), dma((nhalf,)), dma((nhalf,)), dma((nown, chips)),
+            pltpu.VMEM((nhalf, PACK, BLK), F32),
+            pltpu.VMEM((nhalf, PACK, BLK), F32),
+            dma((nhalf,)), dma((nhalf,)), dma((nhalf,)), dma((nhalf,)), dma((nhalf,)),
         ],
         compiler_params=pltpu.CompilerParams(collective_id=0, has_side_effects=True),
         name="reduce_factors",
@@ -371,26 +469,27 @@
         out_specs=(vmem, vmem),
         scratch_shapes=[
             pltpu.VMEM((nblocks, PACK, BLK), F32),
-            dma((nown, chips - 1)), dma((nblocks,)), dma((nhalf,)),
+            dma((nhalf,)), dma((nhalf,)), dma((nblocks,)), dma((nhalf,)),
             dma((nblocks, sections - 1)), dma((sections, nblocks)),
         ],
         compiler_params=pltpu.CompilerParams(collective_id=1, has_side_effects=True),
         name="spread_inverses",
     )(packed)
 
-    per_step = HOST // nblocks
+    group = 2 if nblocks % 2 == 0 else 1
+    per_step = HOST // (nblocks // group)
     precond, held = pl.pallas_call(
         functools.partial(apply_kernel, per_step),
         grid_spec=pltpu.PrefetchScalarGridSpec(
             num_scalar_prefetch=1,
-            grid=(nblocks,),
+            grid=(nblocks // group,),
             in_specs=[
-                pl.BlockSpec((1, BLK, BLK), lambda i, o: (i, 0, 0)),
-                pl.BlockSpec((BLK, columns), lambda i, o: (i, 0)),
+                pl.BlockSpec((group, BLK, BLK), lambda i, o: (i, 0, 0)),
+                pl.BlockSpec((group * BLK, columns), lambda i, o: (i, 0)),
                 pl.BlockSpec((sections, nblocks, share, BLK), lambda i, o: (0, 0, 0, 0), pipeline_mode=pl.Buffered(1)),
             ],
             out_specs=[
-                pl.BlockSpec((BLK, columns), lambda i, o: (i, 0)),
+                pl.BlockSpec((group * BLK, columns), lambda i, o: (i, 0)),
                 pl.BlockSpec((per_step, share, BLK), lambda i, o: (i, 0, 0)),
             ],
             scratch_shapes=[pltpu.SMEM((HOST,), jnp.int32)],

time: 110 us -> 87.6 us (0.80)
  Pallas kernels: 109 us -> 85.7 us
    pallas_call x1, Pallas kernels: 52.6 us -> 32 us  [shards(): pl.pallas_call(functools.partial(spread_kernel, n, sections, nhalf, nown)...]
    pallas_call x1, Pallas kernels: 13.1 us -> 10.5 us  [shards(): pl.pallas_call(functools.partial(apply_kernel, per_step), grid_spec=pltpu...]
where the time goes in v2:
time: 87.6 us; the launch traced here: 86.4 us
  Pallas kernels  85.7 us (98%)
    pallas_call x1, Pallas kernels, shards(): pl.pallas_call(functools.partial(spread_kernel, n, sections, nhalf, nown)...  32 us
    pallas_call x1, Pallas kernels, shards(): pl.pallas_call(functools.partial(invert_kernel, float(tokens * n)), out_s...  22.2 us
    pallas_call x1, Pallas kernels, shards(): pl.pallas_call(functools.partial(reduce_kernel, n, nhalf, nown), out_shap...  21 us
    pallas_call x1, Pallas kernels, shards(): pl.pallas_call(functools.partial(apply_kernel, per_step), grid_spec=pltpu...  10.5 us

profile of v2, /device:TPU:25, one launch (start us, length us, event | category | flops | bytes accessed | tf_op | source)
XLA Modules:
  0.0 86.4 jit_solution(7836971367685182236)
XLA Ops:
  0.6 21.0 %reduce_factors.1.packed = f32[2,136,256]{2,1,0:T(8,128)} custom-call(bf16[256,3072]{1,0:T(8,128)(2,1)} %bitcast.2), custom_call_target="tpu_custom_call" | custom-call | tf_op jit(solution)/shard_map/reduce_factors/pallas_call | solution.py:437
  21.7 22.2 %invert_blocks.1.packed = f32[2,136,256]{2,1,0:T(8,128)} custom-call(f32[2,136,256]{2,1,0:T(8,128)} %reduce_factors.1.packed), custom_call_target="tpu_custom_call" | custom-call | tf_op jit(solution)/shard_map/invert_blocks/pallas_call | solution.py:454
  43.8 32.0 %spread_inverses.1 = (f32[12,256,256]{2,1,0:T(8,128)}, f32[4,12,32,256]{3,2,1,0:T(8,128)}) custom-call(f32[2,136,256]{2,1,0:T(8,128)} %invert_blocks.1.packed), custom_call_target="tpu_custom_call" | custom-call | tf_op jit(solution)/shard_map/spread_inverses/pallas_call | solution.py:462
  75.8 10.5 %apply_inverses.1 = (f32[3072,512]{1,0:T(8,128)}, f32[24,32,256]{2,1,0:T(8,128)}) custom-call(s32[4,12]{1,0:T(4,128)} %owners.1, f32[12,256,256]{2,1,0:T(8,128)} %get-tuple-element.6.inverse, f32[3072,512]{1,0:T(8,128)} %grad.1, f32[4,12,32,256]{3,2,1,0:T(8,128)} %get-tuple-element.7.rows), custom_call_target="tpu_custom_call" | custom-call | tf_op jit(solution)/shard_map/apply_inverses/pallas_call | solution.py:481

commit v3 on v2

--- a/solution.py
+++ b/solution.py
@@ -11,6 +11,7 @@
 HALF = BLK // 2
 PACK = HALF + 8
 HOST = 24
+UNROLL = 1
 MESH = pl.DeviceIdType.MESH
 
 damping_ratio = 0.1
@@ -94,17 +95,7 @@
             device_id={"dp": pair}, device_id_type=MESH,
         )
 
-    @pl.loop(0, nhalf)
-    def _(t):
-        partial(2 * t + 1 - core, theirs.at[t])
-        pair_copy(t).start()
-
-    @pl.loop(0, nhalf)
-    def _(t):
-        partial(2 * t + core, mine.at[t])
-
-    @pl.loop(0, nhalf)
-    def _(t):
+    def fold_pair(t):
         pair_copy(t).wait()
         mine[t] = mine[t] + from_pair[t]
 
@@ -123,13 +114,25 @@
     up = sorted((t for t in range(nhalf) if owners[t] > 0), key=lambda t: -owners[t])
     down = sorted((t for t in range(nhalf) if owners[t] < chips - 1), key=lambda t: owners[t])
 
-    @pl.loop(0, nhalf + chips - 1)
+    turns = sorted(range(nhalf), key=lambda t: (min(up.index(t) if t in up else nhalf, down.index(t) if t in down else nhalf), t))
+
+    @pl.loop(0, nhalf + chips)
     def _(tick):
-        i = tick - chip
+        for turn in (2 * tick, 2 * tick + 1):
+            @pl.when(turn < nhalf)
+            def _():
+                t = look_up(turns, turn)
+                partial(2 * t + 1 - core, theirs.at[t])
+                pair_copy(t).start()
+                partial(2 * t + core, mine.at[t])
+
+        i = tick - 1 - chip
         t = look_up(up, i)
 
         @pl.when((i >= 0) & (i < len(up)) & (look_up(owners, t) > chip))
         def _():
+            fold_pair(t)
+
             @pl.when(chip > 0)
             def _():
                 upward(t).wait_recv()
@@ -137,11 +140,13 @@
 
             upward(t).start()
 
-        j = tick - (chips - 1 - chip)
+        j = tick - 1 - (chips - 1 - chip)
         u = look_up(down, j)
 
         @pl.when((j >= 0) & (j < len(down)) & (look_up(owners, u) < chip))
         def _():
+            fold_pair(u)
+
             @pl.when(chip < chips - 1)
             def _():
                 downward(u).wait_recv()
@@ -155,6 +160,7 @@
 
         @pl.when(t < nhalf)
         def _():
+            fold_pair(t)
             out[slot] = mine[t]
 
             @pl.when(chip > 0)
@@ -193,10 +199,13 @@
     lane = lax.broadcasted_iota(jnp.int32, panel_shape, 2)
     all_lanes = lax.broadcasted_iota(jnp.int32, (count, HALF, HALF), 2)
 
-    def panel(_, a):
+    def columns_of(top, first):
+        return tuple(jnp.broadcast_to(top[:, :, k : k + 1], panel_shape) for k in range(first, first + 8))
+
+    def panel(_, state):
+        a, cols = state
+        cols = list(cols)
         top = a[:, 0:8, :]
-        cols = [jnp.broadcast_to(top[:, :, k : k + 1], panel_shape) for k in range(8)]
-        lead = [jnp.broadcast_to(a[:, :, k : k + 1], a.shape) for k in range(8)]
         for k in range(8):
             here = cols[k]
             inv = jnp.broadcast_to(1.0 / here[:, k : k + 1, :], panel_shape)
@@ -209,16 +218,18 @@
                 across = jnp.broadcast_to(cols[j][:, k : k + 1, :], panel_shape) * inv
                 cols[j] = jnp.where(at_row, across, cols[j] - here * across)
         top = jnp.where(lane < 8, -top, top)
-        rest = a
-        for k in range(8):
-            rest = rest - lead[k] * top[:, k : k + 1, :]
+        rest = a - jnp.stack([
+            lax.dot_general(a[i, 0:8, :], top[i], (((0,), (0,)), ((), ())), precision=HIGHEST, preferred_element_type=F32)
+            for i in range(count)
+        ])
+        ahead = columns_of(rest[:, 8:16, :], 8)
         tall = jnp.concatenate([top, jnp.zeros((count, HALF - 8, HALF), F32)], axis=1)
         turned = jnp.stack([tall[i].T for i in range(count)])
         rest = jnp.where(all_lanes < 8, turned, rest)
         a = jnp.concatenate([rest[:, 8:, :], top], axis=1)
-        return pltpu.roll(a, HALF - 8, 2)
-
-    return -lax.fori_loop(0, HALF // 8, panel, a)
+        return pltpu.roll(a, HALF - 8, 2), ahead
+
+    return -lax.fori_loop(0, HALF // 8, panel, (a, columns_of(a[:, 0:8, :], 0)), unroll=UNROLL)[0]
 
 
 def invert_kernel(tokens, packed, out):

time: 87.6 us -> 81.9 us (0.935)
  Pallas kernels: 85.7 us -> 80.4 us
    pallas_call x1, Pallas kernels: 22.2 us -> 18.1 us  [shards(): pl.pallas_call(functools.partial(invert_kernel, float(tokens * n)), out_s...]
    pallas_call x1, Pallas kernels: 21 us -> 19.8 us  [shards(): pl.pallas_call(functools.partial(reduce_kernel, n, nhalf, nown), out_shap...]
where the time goes in v3:
time: 81.9 us; the launch traced here: 81.1 us
  Pallas kernels  80.4 us (98%)
    pallas_call x1, Pallas kernels, shards(): pl.pallas_call(functools.partial(spread_kernel, n, sections, nhalf, nown)...  32 us
    pallas_call x1, Pallas kernels, shards(): pl.pallas_call(functools.partial(reduce_kernel, n, nhalf, nown), out_shap...  19.8 us
    pallas_call x1, Pallas kernels, shards(): pl.pallas_call(functools.partial(invert_kernel, float(tokens * n)), out_s...  18.1 us
    pallas_call x1, Pallas kernels, shards(): pl.pallas_call(functools.partial(apply_kernel, per_step), grid_spec=pltpu...  10.5 us

profile of v3, /device:TPU:25, one launch (start us, length us, event | category | flops | bytes accessed | tf_op | source)
XLA Modules:
  0.0 81.1 jit_solution(11904422524002790308)
XLA Ops:
  0.6 19.8 %reduce_factors.1.packed = f32[2,136,256]{2,1,0:T(8,128)} custom-call(bf16[256,3072]{1,0:T(8,128)(2,1)} %bitcast.2), custom_call_target="tpu_custom_call" | custom-call | tf_op jit(solution)/shard_map/reduce_factors/pallas_call | solution.py:448
  20.5 18.1 %invert_blocks.1.packed = f32[2,136,256]{2,1,0:T(8,128)} custom-call(f32[2,136,256]{2,1,0:T(8,128)} %reduce_factors.1.packed), custom_call_target="tpu_custom_call" | custom-call | tf_op jit(solution)/shard_map/invert_blocks/pallas_call | solution.py:465
  38.6 32.0 %spread_inverses.1 = (f32[12,256,256]{2,1,0:T(8,128)}, f32[4,12,32,256]{3,2,1,0:T(8,128)}) custom-call(f32[2,136,256]{2,1,0:T(8,128)} %invert_blocks.1.packed), custom_call_target="tpu_custom_call" | custom-call | tf_op jit(solution)/shard_map/spread_inverses/pallas_call | solution.py:473
  70.5 10.5 %apply_inverses.1 = (f32[3072,512]{1,0:T(8,128)}, f32[24,32,256]{2,1,0:T(8,128)}) custom-call(s32[4,12]{1,0:T(4,128)} %owners.1, f32[12,256,256]{2,1,0:T(8,128)} %get-tuple-element.6.inverse, f32[3072,512]{1,0:T(8,128)} %grad.1, f32[4,12,32,256]{3,2,1,0:T(8,128)} %get-tuple-element.7.rows), custom_call_target="tpu_custom_call" | custom-call | tf_op jit(solution)/shard_map/apply_inverses/pallas_call | solution.py:492

commit v4 on v3

--- a/solution.py
+++ b/solution.py
@@ -428,8 +428,9 @@
         a_low = (a - a_high.astype(F32)).astype(BF16)
         b_high = b.astype(BF16)
         b_low = (b - b_high.astype(F32)).astype(BF16)
-        small = jnp.dot(a_high, b_low, preferred_element_type=F32) + jnp.dot(a_low, b_high, preferred_element_type=F32)
-        precond[span, :] = jnp.dot(a_high, b_high, preferred_element_type=F32) + small
+        left = jnp.concatenate([a_high, a_low, a_high], axis=1)
+        right = jnp.concatenate([b_low, b_high, b_high], axis=0)
+        precond[span, :] = jnp.dot(left, right, preferred_element_type=F32)
 
 
 def shards(acts, grad, owner_of):

time: 81.9 us -> 81.9 us (level)
  no operation moved by 1% of the time
where the time goes in v4:
time: 81.9 us; the launch traced here: 81.1 us
  Pallas kernels  80.5 us (98%)
    pallas_call x1, Pallas kernels, shards(): pl.pallas_call(functools.partial(spread_kernel, n, sections, nhalf, nown)...  32 us
    pallas_call x1, Pallas kernels, shards(): pl.pallas_call(functools.partial(reduce_kernel, n, nhalf, nown), out_shap...  19.8 us
    pallas_call x1, Pallas kernels, shards(): pl.pallas_call(functools.partial(invert_kernel, float(tokens * n)), out_s...  18.1 us
    pallas_call x1, Pallas kernels, shards(): pl.pallas_call(functools.partial(apply_kernel, per_step), grid_spec=pltpu...  10.6 us

profile of v4, /device:TPU:25, one launch (start us, length us, event | category | flops | bytes accessed | tf_op | source)
XLA Modules:
  0.0 81.1 jit_solution(15040597519616047845)
XLA Ops:
  0.6 19.8 %reduce_factors.1.packed = f32[2,136,256]{2,1,0:T(8,128)} custom-call(bf16[256,3072]{1,0:T(8,128)(2,1)} %bitcast.2), custom_call_target="tpu_custom_call" | custom-call | tf_op jit(solution)/shard_map/reduce_factors/pallas_call | solution.py:449
  20.5 18.1 %invert_blocks.1.packed = f32[2,136,256]{2,1,0:T(8,128)} custom-call(f32[2,136,256]{2,1,0:T(8,128)} %reduce_factors.1.packed), custom_call_target="tpu_custom_call" | custom-call | tf_op jit(solution)/shard_map/invert_blocks/pallas_call | solution.py:466
  38.6 32.0 %spread_inverses.1 = (f32[12,256,256]{2,1,0:T(8,128)}, f32[4,12,32,256]{3,2,1,0:T(8,128)}) custom-call(f32[2,136,256]{2,1,0:T(8,128)} %invert_blocks.1.packed), custom_call_target="tpu_custom_call" | custom-call | tf_op jit(solution)/shard_map/spread_inverses/pallas_call | solution.py:474
  70.5 10.6 %apply_inverses.1 = (f32[3072,512]{1,0:T(8,128)}, f32[24,32,256]{2,1,0:T(8,128)}) custom-call(s32[4,12]{1,0:T(4,128)} %owners.1, f32[12,256,256]{2,1,0:T(8,128)} %get-tuple-element.6.inverse, f32[3072,512]{1,0:T(8,128)} %grad.1, f32[4,12,32,256]{3,2,1,0:T(8,128)} %get-tuple-element.7.rows), custom_call_target="tpu_custom_call" | custom-call | tf_op jit(solution)/shard_map/apply_inverses/pallas_call | solution.py:493
